TPU v7x, 32 devices: a whole 2x2x4 slice. The times are simulated.
32 devices in a mesh: group: 4 (over y, core), peer: 8 (over z, x).
Axes of the slice: x: 2, y: 2, z: 4, core: 2. Of those that a mesh axis runs over, the one named last changes fastest.
Arguments:
- states: float32 [41, 1048576], P(None, ('group', 'peer')), may hold values from -6 to 6
- block_part: int32 [8192], P(('group', 'peer')), may hold values from 0 to 31, as said below
- tile_perm: int32 [8192, 128], P(('group', 'peer')), may hold values from 0 to 127, each once within a row
- half_volt: float32 [40], replicated, may hold values from -4 to 4
- steepness: float32 [40], replicated, may hold values from 0.5 to 4
- gate_rate: float32 [40], replicated, may hold values from 0.1 to 1
- conductance: float32 [40], replicated, may hold values from 0.005 to 0.08
- reversal: float32 [40], replicated, may hold values from -6 to 6
Outputs:
- regrouped: float32 [41, 1048576], P(None, ('group', 'peer'))
Inputs may be any that keep to these rules, and one draw needn't show every extreme that they name: `block_part`: every partition holds exactly 256 blocks. Within each slab of 256 consecutive global blocks no partition holds more than 16 blocks; every slab has exactly 16 blocks of some partition, and every partition has exactly 16 blocks in some slab.
All inputs are finite; a program needn't handle non-finite values.
Results may differ from a plain program's by a relative error of at most 0.0001.
Values sent between devices are 32-bit elements; how exact they have to be, the bound alone decides.
No kernel may reach another device: no remote copies, remote signals or barrier semaphores. Data moves between devices by JAX's collectives and lax.ppermute only.
A program may use at most 192 MiB of HBM per device.

v0:
```python
import functools

import jax
import jax.numpy as jnp
from jax import lax
from jax.experimental import pallas as pl
from jax.experimental.pallas import tpu as pltpu
from jax.sharding import PartitionSpec as P


time_step = 0.25
sublanes = 8
both = ("group", "peer")
smem_full = pl.BlockSpec(memory_space=pltpu.SMEM)
vmem_full = pl.BlockSpec(memory_space=pltpu.VMEM)
any_full = pl.BlockSpec(memory_space=pl.ANY)


def round_up(value, step):
    return -(-value // step) * step


class Plan:
    def __init__(self, rows, blocks, width):
        self.rows, self.blocks, self.width = rows, blocks, width
        self.peers = lax.axis_size("peer")
        self.devices = lax.axis_size("group") * self.peers
        self.near = self.peers // 2
        self.mates = self.devices // 2
        most = 2 * blocks // self.devices
        self.slots = max(3 * most // 8, 1)
        self.over = most - self.slots
        self.full = rows // sublanes * sublanes
        self.extra = rows - self.full
        self.most = self.slots + self.over
        self.inner_rows = round_up(rows * self.most, sublanes)
        self.cross_rows = round_up(rows * self.slots, sublanes)
        self.relay_rows = round_up(rows * 2 * self.over, sublanes)
        self.side = self.peers // 4
        self.flat = self.devices // 4
        self.worst = self.flat * self.over

    def half(self, device):
        return (device % self.peers) // self.near

    def mate(self, device):
        return device // self.peers * self.near + device % self.near

    def device(self, mate, half):
        return mate // self.near * self.peers + half * self.near + mate % self.near

    def plane(self, device):
        return device % self.peers // self.side

    def spot(self, device):
        return device // self.peers * self.side + device % self.side

    def at(self, spot, plane):
        return spot // self.side * self.peers + plane * self.side + spot % self.side

    def twin(self, device, flip):
        return self.at(self.spot(device), self.plane(device) ^ flip)

    def me(self):
        return lax.axis_index("group") * self.peers + lax.axis_index("peer")


def advanced(params_ref, vals, tail):
    full = vals.shape[0]
    voltage = vals[0:1]
    relax = 1.5 + 0.5 * jnp.tanh(0.5 * voltage)
    done, current = [], 0.0
    for part, rows in ((vals, slice(0, full)), (tail, slice(full, None))):
        if part is None:
            continue
        steady = 0.5 + 0.5 * jnp.tanh((voltage - params_ref[0, rows]) * params_ref[1, rows])
        damping = jnp.exp(params_ref[2, rows] * relax)
        gates = steady + (part - steady) * damping
        drive = params_ref[3, rows] * gates * (voltage - params_ref[4, rows])
        current = current + jnp.sum(drive, axis=0, keepdims=True)
        done.append(gates)
    row = lax.broadcasted_iota(jnp.int32, vals.shape, 0)
    done[0] = jnp.where(row == 0, voltage - time_step * current, done[0])
    return done


def advance_kernel(params_ref, states_ref, out_ref, *, width):
    rows = states_ref.shape[0]
    full = rows // sublanes * sublanes

    lanes = 4 * width if states_ref.shape[1] % (4 * width) == 0 else width

    def one(i, carry):
        for j in range(lanes // width):
            at = pl.multiple_of(i * lanes + j * width, width)
            cols = pl.ds(at, width)
            tail = states_ref[full:rows, cols] if rows > full else None
            done = advanced(params_ref, states_ref[0:full, cols], tail)
            out_ref[0:full, cols] = done[0]
            if rows > full:
                out_ref[full:rows, cols] = done[1]
        return carry

    lax.fori_loop(0, states_ref.shape[1] // lanes, one, 0)


def gate_params(half_volt, steepness, gate_rate, conductance, reversal, width):
    params = jnp.stack([half_volt, 0.5 * steepness, -gate_rate, conductance, reversal])
    params = jnp.pad(params, ((0, 0), (1, 0)))
    return jnp.broadcast_to(params[:, :, None], params.shape + (width,))


def advance(params, states):
    rows, nodes = states.shape
    width = params.shape[2]
    block = fitting(nodes, 4096)
    return pl.pallas_call(
        functools.partial(advance_kernel, width=width),
        grid=(nodes // block,),
        in_specs=[
            pl.BlockSpec(params.shape, lambda i: (0, 0, 0)),
            pl.BlockSpec((rows, block), lambda i: (0, i)),
        ],
        out_specs=pl.BlockSpec((rows, block), lambda i: (0, i)),
        out_shape=jax.ShapeDtypeStruct(states.shape, states.dtype),
        cost_estimate=pl.CostEstimate(
            flops=40 * rows * nodes,
            bytes_accessed=8 * rows * nodes,
            transcendentals=3 * rows * nodes,
        ),
        name="advance",
    )(params, states)


def fitting(total, most):
    size = min(total, most)
    while total % size:
        size -= 128
    return size


def put_block(plan, adv_ref, block, put, base, tail):
    cols = pl.ds(pl.multiple_of(block * plan.width, plan.width), plan.width)
    put(base, plan.full, adv_ref[0 : plan.full, cols])
    for e in range(plan.extra):
        put(tail(e), 1, adv_ref[plan.full + e : plan.full + e + 1, cols])


far_planes = (2, 3)


def dense_kernel(table_ref, states_ref, *outs, plan, room):
    me = plan.me()

    def one(s, carry):
        start, *places = carry
        count = table_ref[s, 0, me]
        flip = plan.plane(s) ^ plan.plane(me)
        spilled = jnp.maximum(count - plan.slots, 0)
        nexts = []
        for far, at, out_ref in zip(far_planes, places, outs):
            more = spilled * (flip == far).astype(jnp.int32)

            def spill(k, carry, at=at, out_ref=out_ref):
                slot = jnp.minimum(at + k, room - 1)

                def put(base, size, vals):
                    if size == plan.full:
                        base = pl.multiple_of(base, sublanes)
                    out_ref[pl.ds(base, size), :] = vals

                put_block(
                    plan,
                    states_ref,
                    start + plan.slots + k,
                    put,
                    slot * plan.full,
                    lambda e: room * plan.full + e * room + slot,
                )
                return carry

            lax.fori_loop(0, more, spill, 0)
            nexts.append(at + more)
        return (start + count, *nexts)

    lax.fori_loop(0, plan.devices, one, (0, 0, 0))


def pack_dense(plan, table, states, room):
    rows = round_up(room * plan.rows, sublanes)
    piece = jax.ShapeDtypeStruct((rows, plan.width), states.dtype)
    return pl.pallas_call(
        functools.partial(dense_kernel, plan=plan, room=room),
        in_specs=[smem_full, vmem_full],
        out_specs=[vmem_full] * 2,
        out_shape=[piece] * 2,
        name="pack_dense",
    )(table, states)


def pieces_kernel(table_ref, adv_ref, *refs, plan, inner, cross):
    outs, start_ref = refs[:-1], refs[-1]
    me = plan.me()
    mine = plan.half(me)
    here = plan.mate(me)

    def scan(s, start):
        start_ref[s] = start
        return start + table_ref[s, 0, me]

    lax.fori_loop(0, plan.devices, scan, 0)
    jobs = [(d, mine, plan.most) for d in inner] + [(d, 1 - mine, plan.slots) for d in cross]
    for (d, half, slots), out_ref in zip(jobs, outs):
        start = start_ref[plan.device(here ^ d, half)]

        def put(base, size, vals):
            out_ref[base : base + size, :] = vals

        for k in range(slots):
            put_block(
                plan,
                adv_ref,
                jnp.minimum(start + k, plan.blocks - 1),
                put,
                k * plan.full,
                lambda e: slots * plan.full + e * slots + k,
            )


def pack_pieces(plan, table, adv, inner, cross):
    rows = [plan.inner_rows] * len(inner) + [plan.cross_rows] * len(cross)
    return pl.pallas_call(
        functools.partial(pieces_kernel, plan=plan, inner=inner, cross=cross),
        in_specs=[smem_full, vmem_full],
        out_specs=[vmem_full] * len(rows),
        out_shape=[jax.ShapeDtypeStruct((size, plan.width), adv.dtype) for size in rows],
        scratch_shapes=[pltpu.SMEM((plan.devices,), jnp.int32)],
    )(table, adv)


def relay_kernel(table_ref, params_ref, *refs, plan, room):
    dense, outs = refs[:2], refs[2 : 2 + plan.flat]
    first_refs, done_refs = refs[2 + plan.flat : 4 + plan.flat], refs[4 + plan.flat :]
    me = plan.me()
    plane = plan.plane(me)
    here = plan.spot(me)
    slots = 2 * plan.over
    for j, far in enumerate(far_planes):
        dense_ref, done_ref, first_ref = dense[j], done_refs[j], first_refs[j]
        source = plan.twin(me, far)

        def scan(t, at):
            first_ref[t] = at
            return at + jnp.maximum(table_ref[plan.at(t, plane), 0, source] - plan.slots, 0)

        total = lax.fori_loop(0, plan.flat, scan, 0)

        def step(i, carry):
            rows = pl.ds(pl.multiple_of(i * plan.full, plan.full), plan.full)
            lasts = [pl.ds(room * plan.full + e * room + i, 1) for e in range(plan.extra)]
            tail = None
            if plan.extra:
                tail = [dense_ref[last, :] for last in lasts]
                tail = jnp.concatenate(tail, axis=0) if plan.extra > 1 else tail[0]
            done = advanced(params_ref, dense_ref[rows, :], tail)
            done_ref[rows, :] = done[0]
            for e, last in enumerate(lasts):
                done_ref[last, :] = done[1][e : e + 1]
            return carry

        lax.fori_loop(0, jnp.minimum(total, room), step, 0)
        for d, out_ref in enumerate(outs):
            at = first_ref[here ^ d]
            for k in range(plan.over):
                slot = jnp.minimum(at + k, room - 1)
                to = j * plan.over + k
                out_ref[to * plan.full : (to + 1) * plan.full, :] = done_ref[
                    pl.ds(pl.multiple_of(slot * plan.full, plan.full), plan.full), :
                ]
                for e in range(plan.extra):
                    row = slots * plan.full + e * slots + to
                    out_ref[row : row + 1, :] = done_ref[
                        pl.ds(room * plan.full + e * room + slot, 1), :
                    ]


def relay(plan, table, params, dense, room):
    piece = jax.ShapeDtypeStruct((plan.relay_rows, plan.width), dense[0].dtype)
    starts = pltpu.SMEM((plan.flat,), jnp.int32)
    blocks = pltpu.VMEM(dense[0].shape, dense[0].dtype)
    return pl.pallas_call(
        functools.partial(relay_kernel, plan=plan, room=room),
        in_specs=[smem_full] + [vmem_full] * 3,
        out_specs=[vmem_full] * plan.flat,
        out_shape=[piece] * plan.flat,
        scratch_shapes=[starts, starts, blocks, blocks],
        name="relay",
    )(table, params, *dense)


def permuted(vals, lanes):
    return jnp.take_along_axis(vals, lanes, axis=1, mode="promise_in_bounds")


def unpack_kernel(base_ref, tail_ref, step_ref, perm_ref, *refs, plan, sizes):
    pieces = refs[: len(sizes)]
    out_ref, got_ref, last_ref, sem = refs[len(sizes) :]
    per_step, width = perm_ref.shape
    first = pl.program_id(0) * per_step

    @pl.when(first == 0)
    def _():
        copies, at = [], 0
        for i, (piece_ref, size) in enumerate(zip(pieces, sizes)):
            rows = pl.ds(at, size)
            copies.append(pltpu.make_async_copy(piece_ref, got_ref.at[rows], sem.at[i]))
            at += size
        for copy in copies:
            copy.start()
        for copy in copies:
            copy.wait()

    for i in range(per_step):
        base = pl.multiple_of(base_ref[first + i], sublanes)
        tail = tail_ref[first + i]
        stride = step_ref[first + i]
        lanes = jnp.broadcast_to(perm_ref[i : i + 1, :], (plan.full, width))
        vals = got_ref[pl.ds(base, plan.full), :]
        out_ref[0 : plan.full, i * width : (i + 1) * width] = permuted(vals, lanes)
        for e in range(plan.extra):
            last_ref[e, i : i + 1, :] = got_ref[pl.ds(tail + e * stride, 1), :]
    for e in range(plan.extra):
        last = permuted(last_ref[e], perm_ref[...])
        for i in range(per_step):
            cols = slice(i * width, (i + 1) * width)
            out_ref[plan.full + e : plan.full + e + 1, cols] = last[i : i + 1, :]


def unpack_early(plan, places, perm, pieces):
    per_step = fitting_blocks(plan.blocks, 16)
    sizes = [piece.shape[0] for piece in pieces]
    dtype = pieces[0].dtype
    return pl.pallas_call(
        functools.partial(unpack_kernel, plan=plan, sizes=sizes),
        grid_spec=pltpu.PrefetchScalarGridSpec(
            num_scalar_prefetch=3,
            grid=(plan.blocks // per_step,),
            in_specs=[pl.BlockSpec((per_step, plan.width), lambda i, *_: (i, 0))]
            + [any_full] * len(pieces),
            out_specs=pl.BlockSpec((plan.rows, per_step * plan.width), lambda i, *_: (0, i)),
            scratch_shapes=[
                pltpu.VMEM((sum(sizes), plan.width), dtype),
                pltpu.VMEM((max(plan.extra, 1), per_step, plan.width), dtype),
                pltpu.SemaphoreType.DMA((len(pieces),)),
            ],
        ),
        out_shape=jax.ShapeDtypeStruct((plan.rows, plan.blocks * plan.width), dtype),
        name="unpack_early",
    )(*places, perm, *pieces)


def late_kernel(
    count_ref, block_ref, base_ref, tail_ref, perm_ref, prior_ref, *refs, plan, group
):
    pieces, (out_ref, got_ref, stage_ref, last_ref, lanes_ref) = refs[:-7], refs[-7:-2]
    load_sem, store_sem = refs[-2:]
    size = plan.cross_rows
    loads = [
        pltpu.make_async_copy(piece_ref, got_ref.at[pl.ds(i * size, size)], load_sem.at[i])
        for i, piece_ref in enumerate(pieces)
    ]
    for load in loads:
        load.start()
    for load in loads:
        load.wait()
    count = count_ref[0]

    def store(i):
        cols = pl.ds(pl.multiple_of(block_ref[i] * plan.width, plan.width), plan.width)
        return pltpu.make_async_copy(
            stage_ref.at[i], out_ref.at[:, cols], store_sem.at[i]
        )

    def some(g, carry):
        for u in range(group):
            i = g * group + u
            lanes = perm_ref[pl.ds(block_ref[i], 1), :]
            lanes_ref[u : u + 1, :] = lanes
            base = pl.multiple_of(base_ref[i], sublanes)
            vals = got_ref[pl.ds(base, plan.full), :]
            wide = jnp.broadcast_to(lanes, (plan.full, plan.width))
            stage_ref[i, 0 : plan.full, :] = permuted(vals, wide)
            for e in range(plan.extra):
                row = tail_ref[i] + e * plan.slots
                last_ref[e, u : u + 1, :] = got_ref[pl.ds(row, 1), :]
        for e in range(plan.extra):
            last = permuted(last_ref[e], lanes_ref[...])
            for u in range(group):
                row = plan.full + e
                stage_ref[g * group + u, row : row + 1, :] = last[u : u + 1, :]
        for u in range(group):
            i = g * group + u

            @pl.when(i < count)
            def _(i=i):
                store(i).start()

        return carry

    lax.fori_loop(0, (count + group - 1) // group, some, 0)

    def finish(i, carry):
        store(i).wait()
        return carry

    lax.fori_loop(0, count, finish, 0)


def unpack_late(plan, late, perm, prior, pieces):
    group = sublanes
    most = round_up(plan.mates * plan.slots, group)
    dtype = prior.dtype
    return pl.pallas_call(
        functools.partial(late_kernel, plan=plan, group=group),
        grid_spec=pltpu.PrefetchScalarGridSpec(
            num_scalar_prefetch=4,
            grid=(1,),
            in_specs=[pl.BlockSpec(perm.shape, lambda i, *_: (0, 0)), any_full]
            + [any_full] * len(pieces),
            out_specs=any_full,
            scratch_shapes=[
                pltpu.VMEM((len(pieces) * plan.cross_rows, plan.width), dtype),
                pltpu.VMEM((most, plan.rows, plan.width), dtype),
                pltpu.VMEM((max(plan.extra, 1), group, plan.width), dtype),
                pltpu.VMEM((group, plan.width), perm.dtype),
                pltpu.SemaphoreType.DMA((len(pieces),)),
                pltpu.SemaphoreType.DMA((most,)),
            ],
        ),
        out_shape=jax.ShapeDtypeStruct(prior.shape, dtype),
        input_output_aliases={5: 0},
        name="unpack_late",
    )(*late, perm, prior, *pieces)


def fitting_blocks(total, most):
    size = min(total, most)
    while total % size:
        size -= 1
    return size


def find_places(plan, block_part, me):
    same = block_part[:, None] == block_part[None, :]
    position = jnp.arange(plan.blocks, dtype=jnp.int32)
    ahead = position[None, :] < position[:, None]
    rank = jnp.sum((same & ahead).astype(jnp.int32), axis=1, dtype=jnp.int32)
    home = plan.half(block_part) == plan.half(me)
    direct = rank < plan.slots
    piece = plan.mate(block_part) ^ plan.mate(me)
    spot = plan.spot(block_part) ^ plan.spot(me)
    relayed = plan.mates * plan.inner_rows + spot * plan.relay_rows
    origin = jnp.where(home, piece * plan.inner_rows, relayed)
    slots = jnp.where(home, plan.most, 2 * plan.over)
    flip = plan.plane(block_part) ^ plan.plane(me)
    shift = jnp.where(flip == far_planes[0], 0, plan.over) - plan.slots
    slot = jnp.where(home, rank, rank + shift)
    late = direct & ~home
    base = jnp.where(late, 0, origin + slot * plan.full)
    tail = jnp.where(late, 0, origin + slots * plan.full + slot)
    early = (base, tail, slots)
    order = jnp.sum((ahead & late[None, :]).astype(jnp.int32), axis=1, dtype=jnp.int32)
    chosen = late[None, :] & (order[None, :] == position[:, None])
    base = piece * plan.cross_rows + rank * plan.full
    tail = piece * plan.cross_rows + plan.slots * plan.full + rank
    count = jnp.sum(late.astype(jnp.int32), dtype=jnp.int32).reshape(1)
    listed = [
        jnp.sum(jnp.where(chosen, vals[None, :], 0), axis=1, dtype=jnp.int32)
        for vals in (position, base, tail)
    ]
    return early, (count, *listed)


def mixed(mates):
    pairs = [(d, mates - 1 - d) for d in range(mates // 2)]
    return [d for pair in pairs[1:] + pairs[:1] for d in pair]


def early_inner(mates, side):
    across = [d for d in mixed(mates) if d & side]
    return across[: len(across) // 2]


def exchange(plan, room, table, states, params, block_part, tile_perm):
    over = range(plan.devices)

    def send(piece, target):
        return lax.ppermute(piece, both, [(i, target(i)) for i in over])

    dense = pack_dense(plan, table, states, room)
    crossed = [
        send(piece, functools.partial(plan.twin, flip=far))
        for far, piece in zip(far_planes, dense)
    ]
    adv = advance(params, states)
    first = early_inner(plan.mates, plan.side)
    second = [d for d in range(plan.mates) if d not in first]
    inner = dict(zip(first, pack_pieces(plan, table, adv, first, [])))
    more = pack_pieces(plan, table, adv, second, list(range(plan.mates)))
    inner.update(zip(second, more))
    cross = list(more[len(second) :])
    again = list(relay(plan, table, params, crossed, room))
    for d in range(plan.mates):
        cross[d] = send(cross[d], lambda i: plan.device(plan.mate(i) ^ d, 1 - plan.half(i)))
        if d:
            inner[d] = send(inner[d], lambda i: plan.device(plan.mate(i) ^ d, plan.half(i)))
    for d in range(1, plan.flat):
        again[d] = send(again[d], lambda i: plan.at(plan.spot(i) ^ d, plan.plane(i)))
    inner = [inner[d] for d in range(plan.mates)]
    early, late = find_places(plan, block_part, plan.me())
    out = unpack_early(plan, early, tile_perm, [*inner, *again])
    return unpack_late(plan, late, tile_perm, out, cross)


def on_device(
    states, block_part, tile_perm, half_volt, steepness, gate_rate, conductance, reversal
):
    blocks, width = tile_perm.shape
    plan = Plan(states.shape[0], blocks, width)
    devices = plan.devices
    ids = jnp.arange(devices, dtype=jnp.int32)
    onehot = (block_part[:, None] == ids[None, :]).astype(jnp.int32)
    counts = jnp.sum(onehot, axis=0, dtype=jnp.int32)
    told = jnp.broadcast_to(counts[None, None, :], (devices, 1, devices))
    table = lax.all_to_all(told, both, split_axis=0, concat_axis=0, tiled=True)
    params = gate_params(half_volt, steepness, gate_rate, conductance, reversal, width)
    spilled = jnp.maximum(table - plan.slots, 0)
    spilled = spilled.reshape(devices // plan.peers, 4, plan.side, devices)
    spilled = jnp.sum(spilled, axis=(0, 2), dtype=jnp.int32)
    across = plan.half(ids)[None, :] != jnp.arange(4, dtype=jnp.int32)[:, None] // 2
    spilled = jnp.max(jnp.where(across, spilled, 0))
    rooms = sorted({round_up(-(-plan.worst * part // 40), 2) for part in (18, 21, 25, 40)})
    choice = sum((spilled > room).astype(jnp.int32) for room in rooms[:-1])
    return lax.switch(
        choice,
        [functools.partial(exchange, plan, room) for room in rooms],
        table,
        states,
        params,
        block_part,
        tile_perm,
    )


def solution(mesh):
    return jax.shard_map(
        on_device,
        mesh=mesh,
        in_specs=(
            P(None, both),
            P(both),
            P(both, None),
            P(),
            P(),
            P(),
            P(),
            P(),
        ),
        out_specs=P(None, both),
        check_vma=False,
    )
```

profile of v0, /device:TPU:25, one launch (start us, length us, event | category | flops | bytes accessed | tf_op | source)
XLA Modules:
  0.0 342.9 jit_solution(14918806882329331980)
XLA Ops:
  1.4 6.2 %all-to-all-start = ((s32[32,1,32]{2,1,0:T(1,128)}), s32[32,1,32]{2,1,0:T(1,128)S(1)}, u32[]{:S(2)}, u32[]{:S(2)}) async-start(s32[32,1,32]{2,1,0:T(1,128)} %broadcast_in_dim.191), calls=%async_computation | async-start | bytes 32768 | tf_op jit(solution)/shard_map/all_to_all | solution.py:535
  14.0 328.7 %conditional.1 = (f32[41,32768]{1,0:T(8,128)}) conditional(s32[]{:T(128)} %clamp.3, (s32[256]{0:T(256)}, f32[5,40]{1,0:T(8,128)S(1)}, f32[41,32768]{1,0:T(8,128)}, s32[32,1,32]{2,1,0:T(1,128)S(1)}, s32[256,128]{1,0:T(8,128)}, /*index=5*/()) %tuple.17, (s32[256]{0:T(256)}, f32[5,40]{1,0:T(8,128)S(1)}, ...), branch_computations={%region_3.10_spmd, %region_10.17_spmd, %region_17.24_spmd, %region... | conditional | flops 54881096 | bytes 94725200 | solution.py:544
  15.0 9.5 %advance.6.adv_ref = f32[41,32768]{1,0:T(8,128)} custom-call(f32[5,41,128]{2,1,0:T(8,128)} %broadcast_in_dim.196.params_ref, f32[41,32768]{1,0:T(8,128)} %get-tuple-element.261.states_ref), custom_call_target="tpu_custom_call" | custom-call | flops 53739520 | bytes 10747904 | tf_op jit(solution)/shard_map/cond/branch_2_fun/advance/pallas_call | solution.py:117
  24.5 6.7 %branch_2_fun.2 = (f32[656,128]{1,0:T(8,128)}, f32[656,128]{1,0:T(8,128)}, f32[656,128]{1,0:T(8,128)}, f32[656,128]{1,0:T(8,128)}, f32[656,128]{1,0:T(8,128)}, /...) custom-call(s32[32,1,32]{2,1,0:T(1,128)S(1)} %get-tuple-element.146., ...), custom_call_target="tpu_custom_call" | custom-call | tf_op jit(solution)/shard_map/cond/branch_2_fun/pallas_call | solution.py:232
  39.7 10.6 %collective-permute-done.104.refs_0_ = f32[248,128]{1,0:T(8,128)S(1)} collective-permute-done((f32[248,128]{1,0:T(8,128)}, f32[248,128]{1,0:T(8,128)S(1)}, u32[]{:S(2)}, u32[]{:S(2)}) %collective-permute-start.104) | collective-permute-done | bytes 127008 | tf_op jit(solution)/shard_map/cond/branch_2_fun/ppermute | solution.py:498
  53.8 4.4 %collective-permute-start.110 = (f32[248,128]{1,0:T(8,128)}, f32[248,128]{1,0:T(8,128)S(1)}, u32[]{:S(2)}, u32[]{:S(2)}) collective-permute-start(f32[248,128]{1,0:T(8,128)} %get-tuple-element.181), channel_id=1, source_target_pairs={{0,14},{1,15},{2,12},{3,13},{4,10},{5,11},{6,8},{7,9},{8,6},{9,7},... | collective-permute-start | bytes 380936 | tf_op jit(solution)/shard_map/cond/branch_2_fun/ppermute | solution.py:498
  58.2 5.9 %pack_dense.6 = (f32[2056,128]{1,0:T(8,128)}, f32[2056,128]{1,0:T(8,128)}) custom-call(s32[32,1,32]{2,1,0:T(1,128)S(1)} %get-tuple-element.146.table_ref, f32[41,32768]{1,0:T(8,128)} %get-tuple-element.261.states_ref), custom_call_target="tpu_custom_call" | custom-call | tf_op jit(solution)/shard_map/cond/branch_2_fun/pack_dense/pallas_call | solution.py:192
  66.5 47.4 %collective-permute-done.108.refs_4_ = f32[248,128]{1,0:T(8,128)S(1)} collective-permute-done((f32[248,128]{1,0:T(8,128)}, f32[248,128]{1,0:T(8,128)S(1)}, u32[]{:S(2)}, u32[]{:S(2)}) %collective-permute-start.108) | collective-permute-done | bytes 127008 | tf_op jit(solution)/shard_map/cond/branch_2_fun/ppermute | solution.py:498
  113.9 3.7 %collective-permute-done.109.refs_5_ = f32[248,128]{1,0:T(8,128)S(1)} collective-permute-done((f32[248,128]{1,0:T(8,128)}, f32[248,128]{1,0:T(8,128)S(1)}, u32[]{:S(2)}, u32[]{:S(2)}) %collective-permute-start.109) | collective-permute-done | bytes 127008 | tf_op jit(solution)/shard_map/cond/branch_2_fun/ppermute | solution.py:498
  121.2 53.3 %collective-permute-start.113 = (f32[248,128]{1,0:T(8,128)}, f32[248,128]{1,0:T(8,128)S(1)}, u32[]{:S(2)}, u32[]{:S(2)}) collective-permute-start(f32[248,128]{1,0:T(8,128)} %get-tuple-element.184), channel_id=1, source_target_pairs={{0,21},{1,20},{2,23},{3,22},{4,17},{5,16},{6,19},{7,18},{8,29},{9,... | collective-permute-start | bytes 380936 | tf_op jit(solution)/shard_map/cond/branch_2_fun/ppermute | solution.py:498
  178.1 4.3 %branch_2_fun.3 = (f32[656,128]{1,0:T(8,128)}, f32[656,128]{1,0:T(8,128)}, f32[656,128]{1,0:T(8,128)}, f32[656,128]{1,0:T(8,128)}) custom-call(s32[32,1,32]{2,1,0:T(1,128)S(1)} %get-tuple-element.146.table_ref, f32[41,32768]{1,0:T(8,128)} %advance.6.adv_ref), custom_call_target="tpu_custom_call" | custom-call | tf_op jit(solution)/shard_map/cond/branch_2_fun/pallas_call | solution.py:232
  187.9 4.1 %collective-permute-done.81.refs_2_ = f32[656,128]{1,0:T(8,128)S(1)} collective-permute-done((f32[656,128]{1,0:T(8,128)}, f32[656,128]{1,0:T(8,128)S(1)}, u32[]{:S(2)}, u32[]{:S(2)}) %collective-permute-start.81) | collective-permute-done | bytes 335904 | tf_op jit(solution)/shard_map/cond/branch_2_fun/ppermute | solution.py:498
  192.0 4.2 %collective-permute-start.84 = (f32[656,128]{1,0:T(8,128)}, f32[656,128]{1,0:T(8,128)}, u32[]{:S(2)}, u32[]{:S(2)}) collective-permute-start(f32[656,128]{1,0:T(8,128)} %get-tuple-element.154), channel_id=1, source_target_pairs={{0,9},{1,8},{2,11},{3,10},{4,13},{5,12},{6,15},{7,14},{8,1},{9,0},... | collective-permute-start | bytes 1007624 | tf_op jit(solution)/shard_map/cond/branch_2_fun/ppermute | solution.py:498
  202.4 4.9 %collective-permute-done.84.refs_5_ = f32[656,128]{1,0:T(8,128)} collective-permute-done((f32[656,128]{1,0:T(8,128)}, f32[656,128]{1,0:T(8,128)}, u32[]{:S(2)}, u32[]{:S(2)}) %collective-permute-start.84) | collective-permute-done | bytes 335904 | tf_op jit(solution)/shard_map/cond/branch_2_fun/ppermute | solution.py:498
  211.9 5.5 %collective-permute-done.86.refs_7_ = f32[656,128]{1,0:T(8,128)} collective-permute-done((f32[656,128]{1,0:T(8,128)}, f32[656,128]{1,0:T(8,128)}, u32[]{:S(2)}, u32[]{:S(2)}) %collective-permute-start.86) | collective-permute-done | bytes 335904 | tf_op jit(solution)/shard_map/cond/branch_2_fun/ppermute | solution.py:498
  217.4 3.8 %collective-permute-start.89 = (f32[656,128]{1,0:T(8,128)}, f32[656,128]{1,0:T(8,128)}, u32[]{:S(2)}, u32[]{:S(2)}) collective-permute-start(f32[656,128]{1,0:T(8,128)} %get-tuple-element.159), channel_id=1, source_target_pairs={{0,18},{1,19},{2,16},{3,17},{4,22},{5,23},{6,20},{7,21},{8,26},{9,... | collective-permute-start | bytes 1007624 | tf_op jit(solution)/shard_map/cond/branch_2_fun/ppermute | solution.py:498
  223.1 6.9 %relay.6 = (f32[824,128]{1,0:T(8,128)}, f32[824,128]{1,0:T(8,128)}, f32[824,128]{1,0:T(8,128)}, f32[824,128]{1,0:T(8,128)}, f32[824,128]{1,0:T(8,128)}, /*index=...) custom-call(s32[32,1,32]{2,1,0:T(1,128)S(1)} %get-tuple-element.146.table_ref, ...), custom_call_target="tpu_custom_call" | custom-call | tf_op jit(solution)/shard_map/cond/branch_2_fun/relay/pallas_call | solution.py:291
  233.7 8.6 %collective-permute-start.98 = (f32[824,128]{1,0:T(8,128)}, f32[824,128]{1,0:T(8,128)S(1)}, u32[]{:S(2)}, u32[]{:S(2)}) collective-permute-start(f32[824,128]{1,0:T(8,128)} %get-tuple-element.169), channel_id=1, source_target_pairs={{0,8},{1,9},{2,10},{3,11},{4,12},{5,13},{6,14},{7,15},{8,0},{9,1},... | collective-permute-start | bytes 1265672 | tf_op jit(solution)/shard_map/cond/branch_2_fun/ppermute | solution.py:498
  244.1 18.8 %collective-permute-done.91.refs_12_ = f32[656,128]{1,0:T(8,128)} collective-permute-done((f32[656,128]{1,0:T(8,128)}, f32[656,128]{1,0:T(8,128)}, u32[]{:S(2)}, u32[]{:S(2)}) %collective-permute-start.91) | collective-permute-done | bytes 335904 | tf_op jit(solution)/shard_map/cond/branch_2_fun/ppermute | solution.py:498
  269.2 5.8 %collective-permute-done.94.refs_15_ = f32[656,128]{1,0:T(8,128)S(1)} collective-permute-done((f32[656,128]{1,0:T(8,128)}, f32[656,128]{1,0:T(8,128)S(1)}, u32[]{:S(2)}, u32[]{:S(2)}) %collective-permute-start.94) | collective-permute-done | bytes 335904 | tf_op jit(solution)/shard_map/cond/branch_2_fun/ppermute | solution.py:498
  284.2 20.1 %collective-permute-start.116 = (f32[248,128]{1,0:T(8,128)}, f32[248,128]{1,0:T(8,128)}, u32[]{:S(2)}, u32[]{:S(2)}) collective-permute-start(f32[248,128]{1,0:T(8,128)} %get-tuple-element.187), channel_id=1, source_target_pairs={{0,28},{1,29},{2,30},{3,31},{4,24},{5,25},{6,26},{7,27},{8,20},{9,... | collective-permute-start | bytes 380936 | tf_op jit(solution)/shard_map/cond/branch_2_fun/ppermute | solution.py:498
  306.7 12.8 %collective-permute-done.102.refs_22_ = f32[824,128]{1,0:T(8,128)S(1)} collective-permute-done((f32[824,128]{1,0:T(8,128)}, f32[824,128]{1,0:T(8,128)S(1)}, u32[]{:S(2)}, u32[]{:S(2)}) %collective-permute-start.102) | collective-permute-done | bytes 421920 | tf_op jit(solution)/shard_map/cond/branch_2_fun/ppermute | solution.py:498
  323.4 12.3 %unpack_early.6.prior_ref = f32[41,32768]{1,0:T(8,128)} custom-call(s32[256]{0:T(256)} %get-tuple-element.317.base_ref, s32[256]{0:T(256)} %get-tuple-element.295.tail_ref, s32[256]{0:T(256)} %get-tuple-element.293.step_ref, s32[256,128]{1,0:T(8,128)S(1)} %copy-done.2, f32[656,128]{1,0:T(8,128)} %get-tuple-element.149.refs_0_, f32[656,128]{1,0:T(8,128)} %copy-done.42, ...), custom_call_target="tpu_custom_call" | custom-call | tf_op jit(solution)/shard_map/cond/branch_2_fun/unpack_early/pallas_call | solution.py:343
  336.4 6.0 %unpack_late.6 = f32[41,32768]{1,0:T(8,128)} custom-call(s32[1]{0:T(128)} %bitcast.2.count_ref, s32[256]{0:T(256)} %get-tuple-element.275.block_ref, s32[256]{0:T(256)} %get-tuple-element.274.base_ref, s32[256]{0:T(256)} %get-tuple-element.273.tail_ref, s32[256,128]{1,0:T(8,128)S(1)} %copy-done.2, ...), custom_call_target="tpu_custom_call", output_to_operand_aliasing={{}: (5, {})} | custom-call | tf_op jit(solution)/shard_map/cond/branch_2_fun/unpack_late/pallas_call | solution.py:423
  (142 shorter events, 73.9 us)
Async XLA Ops:
  33.6 30.5 %collective-permute-start.106 = (f32[248,128]{1,0:T(8,128)}, f32[248,128]{1,0:T(8,128)S(1)}, u32[]{:S(2)}, u32[]{:S(2)}) collective-permute-start(f32[248,128]{1,0:T(8,128)} %get-tuple-element.177), channel_id=1, source_target_pairs={{0,6},{1,7},{2,4},{3,5},{4,2},{5,3},{6,0},{7,1},{8,14},{9,15},{10,... | collective-permute-start | bytes 380936 | tf_op jit(solution)/shard_map/cond/branch_2_fun/ppermute | solution.py:498
  36.7 29.0 %collective-permute-start.107 = (f32[248,128]{1,0:T(8,128)}, f32[248,128]{1,0:T(8,128)S(1)}, u32[]{:S(2)}, u32[]{:S(2)}) collective-permute-start(f32[248,128]{1,0:T(8,128)} %get-tuple-element.178), channel_id=1, source_target_pairs={{0,7},{1,6},{2,5},{3,4},{4,3},{5,2},{6,1},{7,0},{8,15},{9,14},{10,... | collective-permute-start | bytes 380936 | tf_op jit(solution)/shard_map/cond/branch_2_fun/ppermute | solution.py:498
  37.8 76.1 %collective-permute-start.108 = (f32[248,128]{1,0:T(8,128)}, f32[248,128]{1,0:T(8,128)S(1)}, u32[]{:S(2)}, u32[]{:S(2)}) collective-permute-start(f32[248,128]{1,0:T(8,128)} %get-tuple-element.179), channel_id=1, source_target_pairs={{0,12},{1,13},{2,14},{3,15},{4,8},{5,9},{6,10},{7,11},{8,4},{9,5},... | collective-permute-start | bytes 380936 | tf_op jit(solution)/shard_map/cond/branch_2_fun/ppermute | solution.py:498
  50.3 67.3 %collective-permute-start.109 = (f32[248,128]{1,0:T(8,128)}, f32[248,128]{1,0:T(8,128)S(1)}, u32[]{:S(2)}, u32[]{:S(2)}) collective-permute-start(f32[248,128]{1,0:T(8,128)} %get-tuple-element.180), channel_id=1, source_target_pairs={{0,13},{1,12},{2,15},{3,14},{4,9},{5,8},{6,11},{7,10},{8,5},{9,4},... | collective-permute-start | bytes 380936 | tf_op jit(solution)/shard_map/cond/branch_2_fun/ppermute | solution.py:498
  53.8 63.9 %collective-permute-start.110 = (f32[248,128]{1,0:T(8,128)}, f32[248,128]{1,0:T(8,128)S(1)}, u32[]{:S(2)}, u32[]{:S(2)}) collective-permute-start(f32[248,128]{1,0:T(8,128)} %get-tuple-element.181), channel_id=1, source_target_pairs={{0,14},{1,15},{2,12},{3,13},{4,10},{5,11},{6,8},{7,9},{8,6},{9,7},... | collective-permute-start | bytes 380936 | tf_op jit(solution)/shard_map/cond/branch_2_fun/ppermute | solution.py:498
  64.8 156.4 %collective-permute-start.95 = (f32[2056,128]{1,0:T(8,128)}, f32[2056,128]{1,0:T(8,128)S(1)}, u32[]{:S(2)}, u32[]{:S(2)}) collective-permute-start(f32[2056,128]{1,0:T(8,128)} %get-tuple-element.165), channel_id=1, source_target_pairs={{0,4},{1,5},{2,6},{3,7},{4,0},{5,1},{6,2},{7,3},{8,12},{9,13},{10,... | collective-permute-start | bytes 3158024 | tf_op jit(solution)/shard_map/cond/branch_2_fun/ppermute | solution.py:498
  66.3 154.9 %collective-permute-start.96 = (f32[2056,128]{1,0:T(8,128)}, f32[2056,128]{1,0:T(8,128)S(1)}, u32[]{:S(2)}, u32[]{:S(2)}) collective-permute-start(f32[2056,128]{1,0:T(8,128)} %get-tuple-element.166), channel_id=1, source_target_pairs={{0,6},{1,7},{2,4},{3,5},{4,2},{5,3},{6,0},{7,1},{8,14},{9,15},{10,... | collective-permute-start | bytes 3158024 | tf_op jit(solution)/shard_map/cond/branch_2_fun/ppermute | solution.py:498
  117.7 56.8 %collective-permute-start.112 = (f32[248,128]{1,0:T(8,128)}, f32[248,128]{1,0:T(8,128)S(1)}, u32[]{:S(2)}, u32[]{:S(2)}) collective-permute-start(f32[248,128]{1,0:T(8,128)} %get-tuple-element.183), channel_id=1, source_target_pairs={{0,20},{1,21},{2,22},{3,23},{4,16},{5,17},{6,18},{7,19},{8,28},{9,... | collective-permute-start | bytes 380936 | tf_op jit(solution)/shard_map/cond/branch_2_fun/ppermute | solution.py:498
  117.7 69.1 %collective-permute-start.80 = (f32[656,128]{1,0:T(8,128)}, f32[656,128]{1,0:T(8,128)S(1)}, u32[]{:S(2)}, u32[]{:S(2)}) collective-permute-start(f32[656,128]{1,0:T(8,128)} %get-tuple-element.150), channel_id=1, source_target_pairs={{0,1},{1,0},{2,3},{3,2},{4,5},{5,4},{6,7},{7,6},{8,9},{9,8},{10,11... | collective-permute-start | bytes 1007624 | tf_op jit(solution)/shard_map/cond/branch_2_fun/ppermute | solution.py:498
  121.2 62.4 %collective-permute-start.113 = (f32[248,128]{1,0:T(8,128)}, f32[248,128]{1,0:T(8,128)S(1)}, u32[]{:S(2)}, u32[]{:S(2)}) collective-permute-start(f32[248,128]{1,0:T(8,128)} %get-tuple-element.184), channel_id=1, source_target_pairs={{0,21},{1,20},{2,23},{3,22},{4,17},{5,16},{6,19},{7,18},{8,29},{9,... | collective-permute-start | bytes 380936 | tf_op jit(solution)/shard_map/cond/branch_2_fun/ppermute | solution.py:498
  207.3 22.8 %collective-permute-start.87 = (f32[656,128]{1,0:T(8,128)}, f32[656,128]{1,0:T(8,128)}, u32[]{:S(2)}, u32[]{:S(2)}) collective-permute-start(f32[656,128]{1,0:T(8,128)} %get-tuple-element.157), channel_id=1, source_target_pairs={{0,16},{1,17},{2,18},{3,19},{4,20},{5,21},{6,22},{7,23},{8,24},{9,... | collective-permute-start | bytes 1007624 | tf_op jit(solution)/shard_map/cond/branch_2_fun/ppermute | solution.py:498
  209.0 24.7 %collective-permute-start.88 = (f32[656,128]{1,0:T(8,128)}, f32[656,128]{1,0:T(8,128)}, u32[]{:S(2)}, u32[]{:S(2)}) collective-permute-start(f32[656,128]{1,0:T(8,128)} %get-tuple-element.158), channel_id=1, source_target_pairs={{0,17},{1,16},{2,19},{3,18},{4,21},{5,20},{6,23},{7,22},{8,25},{9,... | collective-permute-start | bytes 1007624 | tf_op jit(solution)/shard_map/cond/branch_2_fun/ppermute | solution.py:498
  217.4 25.1 %collective-permute-start.89 = (f32[656,128]{1,0:T(8,128)}, f32[656,128]{1,0:T(8,128)}, u32[]{:S(2)}, u32[]{:S(2)}) collective-permute-start(f32[656,128]{1,0:T(8,128)} %get-tuple-element.159), channel_id=1, source_target_pairs={{0,18},{1,19},{2,16},{3,17},{4,22},{5,23},{6,20},{7,21},{8,26},{9,... | collective-permute-start | bytes 1007624 | tf_op jit(solution)/shard_map/cond/branch_2_fun/ppermute | solution.py:498
  221.2 22.9 %collective-permute-start.90 = (f32[656,128]{1,0:T(8,128)}, f32[656,128]{1,0:T(8,128)}, u32[]{:S(2)}, u32[]{:S(2)}) collective-permute-start(f32[656,128]{1,0:T(8,128)} %get-tuple-element.160), channel_id=1, source_target_pairs={{0,19},{1,18},{2,17},{3,16},{4,23},{5,22},{6,21},{7,20},{8,27},{9,... | collective-permute-start | bytes 1007624 | tf_op jit(solution)/shard_map/cond/branch_2_fun/ppermute | solution.py:498
  221.3 41.7 %collective-permute-start.91 = (f32[656,128]{1,0:T(8,128)}, f32[656,128]{1,0:T(8,128)}, u32[]{:S(2)}, u32[]{:S(2)}) collective-permute-start(f32[656,128]{1,0:T(8,128)} %get-tuple-element.161), channel_id=1, source_target_pairs={{0,24},{1,25},{2,26},{3,27},{4,28},{5,29},{6,30},{7,31},{8,16},{9,... | collective-permute-start | bytes 1007624 | tf_op jit(solution)/shard_map/cond/branch_2_fun/ppermute | solution.py:498
  230.1 46.4 %collective-permute-start.97 = (f32[824,128]{1,0:T(8,128)}, f32[824,128]{1,0:T(8,128)S(1)}, u32[]{:S(2)}, u32[]{:S(2)}) collective-permute-start(f32[824,128]{1,0:T(8,128)} %get-tuple-element.168), channel_id=1, source_target_pairs={{0,1},{1,0},{2,3},{3,2},{4,5},{5,4},{6,7},{7,6},{8,9},{9,8},{10,11... | collective-permute-start | bytes 1265672 | tf_op jit(solution)/shard_map/cond/branch_2_fun/ppermute | solution.py:498
  233.7 43.2 %collective-permute-start.98 = (f32[824,128]{1,0:T(8,128)}, f32[824,128]{1,0:T(8,128)S(1)}, u32[]{:S(2)}, u32[]{:S(2)}) collective-permute-start(f32[824,128]{1,0:T(8,128)} %get-tuple-element.169), channel_id=1, source_target_pairs={{0,8},{1,9},{2,10},{3,11},{4,12},{5,13},{6,14},{7,15},{8,0},{9,1},... | collective-permute-start | bytes 1265672 | tf_op jit(solution)/shard_map/cond/branch_2_fun/ppermute | solution.py:498
  244.1 22.6 %collective-permute-start.93 = (f32[656,128]{1,0:T(8,128)}, f32[656,128]{1,0:T(8,128)S(1)}, u32[]{:S(2)}, u32[]{:S(2)}) collective-permute-start(f32[656,128]{1,0:T(8,128)} %get-tuple-element.163), channel_id=1, source_target_pairs={{0,26},{1,27},{2,24},{3,25},{4,30},{5,31},{6,28},{7,29},{8,18},{9,... | collective-permute-start | bytes 1007624 | tf_op jit(solution)/shard_map/cond/branch_2_fun/ppermute | solution.py:498
  275.8 28.6 %collective-permute-start.101 = (f32[824,128]{1,0:T(8,128)}, f32[824,128]{1,0:T(8,128)S(1)}, u32[]{:S(2)}, u32[]{:S(2)}) collective-permute-start(f32[824,128]{1,0:T(8,128)} %get-tuple-element.172), channel_id=1, source_target_pairs={{0,17},{1,16},{2,19},{3,18},{4,21},{5,20},{6,23},{7,22},{8,25},{9,... | collective-permute-start | bytes 1265672 | tf_op jit(solution)/shard_map/cond/branch_2_fun/ppermute | solution.py:498
  276.5 43.0 %collective-permute-start.102 = (f32[824,128]{1,0:T(8,128)}, f32[824,128]{1,0:T(8,128)S(1)}, u32[]{:S(2)}, u32[]{:S(2)}) collective-permute-start(f32[824,128]{1,0:T(8,128)} %get-tuple-element.173), channel_id=1, source_target_pairs={{0,24},{1,25},{2,26},{3,27},{4,28},{5,29},{6,30},{7,31},{8,16},{9,... | collective-permute-start | bytes 1265672 | tf_op jit(solution)/shard_map/cond/branch_2_fun/ppermute | solution.py:498
  276.9 42.6 %collective-permute-start.103 = (f32[824,128]{1,0:T(8,128)}, f32[824,128]{1,0:T(8,128)S(1)}, u32[]{:S(2)}, u32[]{:S(2)}) collective-permute-start(f32[824,128]{1,0:T(8,128)} %get-tuple-element.174), channel_id=1, source_target_pairs={{0,25},{1,24},{2,27},{3,26},{4,29},{5,28},{6,31},{7,30},{8,17},{9,... | collective-permute-start | bytes 1265672 | tf_op jit(solution)/shard_map/cond/branch_2_fun/ppermute | solution.py:498
  282.3 53.4 %collective-permute-start.115 = (f32[248,128]{1,0:T(8,128)}, f32[248,128]{1,0:T(8,128)S(1)}, u32[]{:S(2)}, u32[]{:S(2)}) collective-permute-start(f32[248,128]{1,0:T(8,128)} %get-tuple-element.186), channel_id=1, source_target_pairs={{0,23},{1,22},{2,21},{3,20},{4,19},{5,18},{6,17},{7,16},{8,31},{9,... | collective-permute-start | bytes 380936 | tf_op jit(solution)/shard_map/cond/branch_2_fun/ppermute | solution.py:498
  284.2 51.5 %collective-permute-start.116 = (f32[248,128]{1,0:T(8,128)}, f32[248,128]{1,0:T(8,128)}, u32[]{:S(2)}, u32[]{:S(2)}) collective-permute-start(f32[248,128]{1,0:T(8,128)} %get-tuple-element.187), channel_id=1, source_target_pairs={{0,28},{1,29},{2,30},{3,31},{4,24},{5,25},{6,26},{7,27},{8,20},{9,... | collective-permute-start | bytes 380936 | tf_op jit(solution)/shard_map/cond/branch_2_fun/ppermute | solution.py:498
  304.4 31.4 %collective-permute-start.117 = (f32[248,128]{1,0:T(8,128)}, f32[248,128]{1,0:T(8,128)}, u32[]{:S(2)}, u32[]{:S(2)}) collective-permute-start(f32[248,128]{1,0:T(8,128)} %get-tuple-element.188), channel_id=1, source_target_pairs={{0,29},{1,28},{2,31},{3,30},{4,25},{5,24},{6,27},{7,26},{8,21},{9,... | collective-permute-start | bytes 380936 | tf_op jit(solution)/shard_map/cond/branch_2_fun/ppermute | solution.py:498
  (46 other events, 1551.2 us)
where the time goes:
time: 346 us; the launch traced here: 343 us
  starting transfers between devices  151 us (44%)
  waiting for transfers between devices  124 us (36%)
  Pallas kernels  51.7 us (15%)
  local copies, waits for them, and re-layouts  7.55 us (2%)
  other arithmetic  5.7 us (2%)
    ppermute x40, starting transfers between devices, send(): return lax.ppermute(piece, both, [(i, target(i)) for i in over])  144 us
    ppermute x40, waiting for transfers between devices, send(): return lax.ppermute(piece, both, [(i, target(i)) for i in over])  122 us
    pallas_call x1, Pallas kernels, unpack_early(): pl.pallas_call(functools.partial(unpack_kernel, plan=plan, sizes=sizes),...  12.3 us
    pallas_call x2, Pallas kernels, pack_pieces(): pl.pallas_call(functools.partial(pieces_kernel, plan=plan, inner=inner, c...  11 us
    pallas_call x1, Pallas kernels, advance(): pl.pallas_call(functools.partial(advance_kernel, width=width), grid=(node...  9.46 us
    pallas_call x1, Pallas kernels, relay(): pl.pallas_call(functools.partial(relay_kernel, plan=plan, room=room), in_...  6.94 us
  transfers between devices with their start and end apart: 41, of which 16 were waited for; matrix products, arithmetic and copies ran while one was open for 1% of the time, Pallas kernels for 9%

commit v1 on v0

--- a/solution.py
+++ b/solution.py
@@ -487,8 +487,7 @@
 
 
 def early_inner(mates, side):
-    across = [d for d in mixed(mates) if d & side]
-    return across[: len(across) // 2]
+    return [d for d in mixed(mates) if d & side]
 
 
 def exchange(plan, room, table, states, params, block_part, tile_perm):
@@ -539,7 +538,7 @@
     spilled = jnp.sum(spilled, axis=(0, 2), dtype=jnp.int32)
     across = plan.half(ids)[None, :] != jnp.arange(4, dtype=jnp.int32)[:, None] // 2
     spilled = jnp.max(jnp.where(across, spilled, 0))
-    rooms = sorted({round_up(-(-plan.worst * part // 40), 2) for part in (18, 21, 25, 40)})
+    rooms = sorted({round_up(-(-plan.worst * part // 40), 2) for part in (17, 20, 23, 27, 40)})
     choice = sum((spilled > room).astype(jnp.int32) for room in rooms[:-1])
     return lax.switch(
         choice,

time: 346 us -> 342 us (0.988)
  waiting for transfers between devices: 124 us -> 110 us
  starting transfers between devices: 151 us -> 158 us
    ppermute x40, waiting for transfers between devices: 122 us -> 107 us  [send(): return lax.ppermute(piece, both, [(i, target(i)) for i in over])]
    ppermute x40, starting transfers between devices: 144 us -> 152 us  [send(): return lax.ppermute(piece, both, [(i, target(i)) for i in over])]
  transfers between devices with their start and end apart: 41 -> 41, of which waited for: 16 -> 14; matrix products, arithmetic and copies ran while one was open for 1% -> 1% of each run, Pallas kernels for 9% -> 9%
where the time goes in v1:
time: 342 us; the launch traced here: 336 us
  starting transfers between devices  158 us (46%)
  waiting for transfers between devices  110 us (32%)
  Pallas kernels  51.5 us (15%)
  local copies, waits for them, and re-layouts  7.58 us (2%)
  other arithmetic  5.69 us (2%)
    ppermute x40, starting transfers between devices, send(): return lax.ppermute(piece, both, [(i, target(i)) for i in over])  152 us
    ppermute x40, waiting for transfers between devices, send(): return lax.ppermute(piece, both, [(i, target(i)) for i in over])  107 us
    pallas_call x1, Pallas kernels, unpack_early(): pl.pallas_call(functools.partial(unpack_kernel, plan=plan, sizes=sizes),...  12.3 us
    pallas_call x2, Pallas kernels, pack_pieces(): pl.pallas_call(functools.partial(pieces_kernel, plan=plan, inner=inner, c...  10.9 us
    pallas_call x1, Pallas kernels, advance(): pl.pallas_call(functools.partial(advance_kernel, width=width), grid=(node...  9.46 us
    pallas_call x1, Pallas kernels, relay(): pl.pallas_call(functools.partial(relay_kernel, plan=plan, room=room), in_...  6.91 us
  transfers between devices with their start and end apart: 41, of which 14 were waited for; matrix products, arithmetic and copies ran while one was open for 1% of the time, Pallas kernels for 9%

profile of v1, /device:TPU:25, one launch (start us, length us, event | category | flops | bytes accessed | tf_op | source)
XLA Modules:
  0.0 335.9 jit_solution(3185002545992534604)
XLA Ops:
  1.4 6.2 %all-to-all-start = ((s32[32,1,32]{2,1,0:T(1,128)}), s32[32,1,32]{2,1,0:T(1,128)S(1)}, u32[]{:S(2)}, u32[]{:S(2)}) async-start(s32[32,1,32]{2,1,0:T(1,128)} %broadcast_in_dim.232), calls=%async_computation | async-start | bytes 32768 | tf_op jit(solution)/shard_map/all_to_all | solution.py:534
  14.6 321.0 %conditional.1 = (f32[41,32768]{1,0:T(8,128)}) conditional(s32[]{:T(128)} %clamp.3, (s32[256]{0:T(256)}, f32[5,40]{1,0:T(8,128)S(1)}, f32[41,32768]{1,0:T(8,128)}, s32[32,1,32]{2,1,0:T(1,128)S(1)}, s32[256,128]{1,0:T(8,128)}, /*index=5*/()) %tuple.20, (s32[256]{0:T(256)}, f32[5,40]{1,0:T(8,128)S(1)}, ...), branch_computations={%region_3.10_spmd, %region_10.17_spmd, %region_17.24_spmd, %region... | conditional | flops 54881096 | bytes 94725200 | solution.py:543
  15.7 9.5 %advance.7.adv_ref = f32[41,32768]{1,0:T(8,128)} custom-call(f32[5,41,128]{2,1,0:T(8,128)} %broadcast_in_dim.237.params_ref, f32[41,32768]{1,0:T(8,128)} %get-tuple-element.324.states_ref), custom_call_target="tpu_custom_call" | custom-call | flops 53739520 | bytes 10747904 | tf_op jit(solution)/shard_map/cond/branch_2_fun/advance/pallas_call | solution.py:117
  25.2 6.0 %branch_2_fun.2 = (f32[656,128]{1,0:T(8,128)}, f32[656,128]{1,0:T(8,128)}, f32[656,128]{1,0:T(8,128)}, f32[656,128]{1,0:T(8,128)}, f32[656,128]{1,0:T(8,128)}, /...) custom-call(s32[32,1,32]{2,1,0:T(1,128)S(1)} %get-tuple-element.157., ...), custom_call_target="tpu_custom_call" | custom-call | tf_op jit(solution)/shard_map/cond/branch_2_fun/pallas_call | solution.py:232
  39.7 10.6 %collective-permute-done.104.refs_0_ = f32[248,128]{1,0:T(8,128)S(1)} collective-permute-done((f32[248,128]{1,0:T(8,128)}, f32[248,128]{1,0:T(8,128)S(1)}, u32[]{:S(2)}, u32[]{:S(2)}) %collective-permute-start.104) | collective-permute-done | bytes 127008 | tf_op jit(solution)/shard_map/cond/branch_2_fun/ppermute | solution.py:497
  53.1 4.4 %collective-permute-start.110 = (f32[248,128]{1,0:T(8,128)}, f32[248,128]{1,0:T(8,128)S(1)}, u32[]{:S(2)}, u32[]{:S(2)}) collective-permute-start(f32[248,128]{1,0:T(8,128)} %get-tuple-element.192), channel_id=1, source_target_pairs={{0,14},{1,15},{2,12},{3,13},{4,10},{5,11},{6,8},{7,9},{8,6},{9,7},... | collective-permute-start | bytes 380936 | tf_op jit(solution)/shard_map/cond/branch_2_fun/ppermute | solution.py:497
  64.3 7.2 %collective-permute-done.108.refs_4_ = f32[248,128]{1,0:T(8,128)S(1)} collective-permute-done((f32[248,128]{1,0:T(8,128)}, f32[248,128]{1,0:T(8,128)S(1)}, u32[]{:S(2)}, u32[]{:S(2)}) %collective-permute-start.108) | collective-permute-done | bytes 127008 | tf_op jit(solution)/shard_map/cond/branch_2_fun/ppermute | solution.py:497
  73.8 5.8 %pack_dense.7 = (f32[1888,128]{1,0:T(8,128)}, f32[1888,128]{1,0:T(8,128)}) custom-call(s32[32,1,32]{2,1,0:T(1,128)S(1)} %get-tuple-element.157.table_ref, f32[41,32768]{1,0:T(8,128)} %get-tuple-element.324.states_ref), custom_call_target="tpu_custom_call" | custom-call | tf_op jit(solution)/shard_map/cond/branch_2_fun/pack_dense/pallas_call | solution.py:192
  86.5 45.5 %collective-permute-start.114 = (f32[248,128]{1,0:T(8,128)S(1)}, f32[248,128]{1,0:T(8,128)S(1)}, u32[]{:S(2)}, u32[]{:S(2)}) collective-permute-start(f32[248,128]{1,0:T(8,128)S(1)} %copy-done.131), channel_id=1, source_target_pairs={{0,22},{1,23},{2,20},{3,21},{4,18},{5,19},{6,16},{7,17},{8,30},{9,... | collective-permute-start | bytes 380936 | tf_op jit(solution)/shard_map/cond/branch_2_fun/ppermute | solution.py:497
  132.0 4.9 %branch_2_fun.3 = (f32[656,128]{1,0:T(8,128)}, f32[656,128]{1,0:T(8,128)}, f32[656,128]{1,0:T(8,128)}, f32[656,128]{1,0:T(8,128)}, f32[656,128]{1,0:T(8,128)}, /...) custom-call(s32[32,1,32]{2,1,0:T(1,128)S(1)} %get-tuple-element.157.table_ref, f32[41,32768]{1,0:T(8,128)} %advance.7.adv_ref), custom_call_target="tpu_custom_call" | custom-call | tf_op jit(solution)/shard_map/cond/branch_2_fun/pallas_call | solution.py:232
  136.9 37.2 %collective-permute-done.113.refs_9_ = f32[248,128]{1,0:T(8,128)S(1)} collective-permute-done((f32[248,128]{1,0:T(8,128)S(1)}, f32[248,128]{1,0:T(8,128)S(1)}, u32[]{:S(2)}, u32[]{:S(2)}) %collective-permute-start.113) | collective-permute-done | bytes 127008 | tf_op jit(solution)/shard_map/cond/branch_2_fun/ppermute | solution.py:497
  182.3 6.6 %collective-permute-start.84 = (f32[656,128]{1,0:T(8,128)}, f32[656,128]{1,0:T(8,128)}, u32[]{:S(2)}, u32[]{:S(2)}) collective-permute-start(f32[656,128]{1,0:T(8,128)} %get-tuple-element.165), channel_id=1, source_target_pairs={{0,9},{1,8},{2,11},{3,10},{4,13},{5,12},{6,15},{7,14},{8,1},{9,0},... | collective-permute-start | bytes 1007624 | tf_op jit(solution)/shard_map/cond/branch_2_fun/ppermute | solution.py:497
  194.5 5.9 %collective-permute-done.84.refs_5_ = f32[656,128]{1,0:T(8,128)} collective-permute-done((f32[656,128]{1,0:T(8,128)}, f32[656,128]{1,0:T(8,128)}, u32[]{:S(2)}, u32[]{:S(2)}) %collective-permute-start.84) | collective-permute-done | bytes 335904 | tf_op jit(solution)/shard_map/cond/branch_2_fun/ppermute | solution.py:497
  203.1 7.5 %collective-permute-done.86.refs_7_ = f32[656,128]{1,0:T(8,128)} collective-permute-done((f32[656,128]{1,0:T(8,128)}, f32[656,128]{1,0:T(8,128)}, u32[]{:S(2)}, u32[]{:S(2)}) %collective-permute-start.86) | collective-permute-done | bytes 335904 | tf_op jit(solution)/shard_map/cond/branch_2_fun/ppermute | solution.py:497
  215.9 6.9 %relay.7 = (f32[824,128]{1,0:T(8,128)}, f32[824,128]{1,0:T(8,128)}, f32[824,128]{1,0:T(8,128)}, f32[824,128]{1,0:T(8,128)}, f32[824,128]{1,0:T(8,128)}, /*index=...) custom-call(s32[32,1,32]{2,1,0:T(1,128)S(1)} %get-tuple-element.157.table_ref, ...), custom_call_target="tpu_custom_call" | custom-call | tf_op jit(solution)/shard_map/cond/branch_2_fun/relay/pallas_call | solution.py:291
  224.6 11.1 %collective-permute-start.92 = (f32[656,128]{1,0:T(8,128)}, f32[656,128]{1,0:T(8,128)S(1)}, u32[]{:S(2)}, u32[]{:S(2)}) collective-permute-start(f32[656,128]{1,0:T(8,128)} %get-tuple-element.173), channel_id=1, source_target_pairs={{0,25},{1,24},{2,27},{3,26},{4,29},{5,28},{6,31},{7,30},{8,17},{9,... | collective-permute-start | bytes 1007624 | tf_op jit(solution)/shard_map/cond/branch_2_fun/ppermute | solution.py:497
  235.7 18.7 %collective-permute-done.91.refs_12_ = f32[656,128]{1,0:T(8,128)} collective-permute-done((f32[656,128]{1,0:T(8,128)}, f32[656,128]{1,0:T(8,128)}, u32[]{:S(2)}, u32[]{:S(2)}) %collective-permute-start.91) | collective-permute-done | bytes 335904 | tf_op jit(solution)/shard_map/cond/branch_2_fun/ppermute | solution.py:497
  260.3 6.1 %collective-permute-done.94.refs_15_ = f32[656,128]{1,0:T(8,128)S(1)} collective-permute-done((f32[656,128]{1,0:T(8,128)}, f32[656,128]{1,0:T(8,128)S(1)}, u32[]{:S(2)}, u32[]{:S(2)}) %collective-permute-start.94) | collective-permute-done | bytes 335904 | tf_op jit(solution)/shard_map/cond/branch_2_fun/ppermute | solution.py:497
  275.2 4.9 %collective-permute-start.115 = (f32[248,128]{1,0:T(8,128)}, f32[248,128]{1,0:T(8,128)S(1)}, u32[]{:S(2)}, u32[]{:S(2)}) collective-permute-start(f32[248,128]{1,0:T(8,128)} %get-tuple-element.197), channel_id=1, source_target_pairs={{0,23},{1,22},{2,21},{3,20},{4,19},{5,18},{6,17},{7,16},{8,31},{9,... | collective-permute-start | bytes 380936 | tf_op jit(solution)/shard_map/cond/branch_2_fun/ppermute | solution.py:497
  280.1 21.4 %collective-permute-start.116 = (f32[248,128]{1,0:T(8,128)}, f32[248,128]{1,0:T(8,128)}, u32[]{:S(2)}, u32[]{:S(2)}) collective-permute-start(f32[248,128]{1,0:T(8,128)} %get-tuple-element.198), channel_id=1, source_target_pairs={{0,28},{1,29},{2,30},{3,31},{4,24},{5,25},{6,26},{7,27},{8,20},{9,... | collective-permute-start | bytes 380936 | tf_op jit(solution)/shard_map/cond/branch_2_fun/ppermute | solution.py:497
  301.5 5.3 %collective-permute-done.102.refs_22_ = f32[824,128]{1,0:T(8,128)S(1)} collective-permute-done((f32[824,128]{1,0:T(8,128)}, f32[824,128]{1,0:T(8,128)S(1)}, u32[]{:S(2)}, u32[]{:S(2)}) %collective-permute-start.102) | collective-permute-done | bytes 421920 | tf_op jit(solution)/shard_map/cond/branch_2_fun/ppermute | solution.py:497
  306.8 8.1 %collective-permute-start.118 = (f32[248,128]{1,0:T(8,128)}, f32[248,128]{1,0:T(8,128)}, u32[]{:S(2)}, u32[]{:S(2)}) collective-permute-start(f32[248,128]{1,0:T(8,128)} %get-tuple-element.200), channel_id=1, source_target_pairs={{0,30},{1,31},{2,28},{3,29},{4,26},{5,27},{6,24},{7,25},{8,22},{9,... | collective-permute-start | bytes 380936 | tf_op jit(solution)/shard_map/cond/branch_2_fun/ppermute | solution.py:497
  316.2 12.3 %unpack_early.7.prior_ref = f32[41,32768]{1,0:T(8,128)} custom-call(s32[256]{0:T(256)} %get-tuple-element.392.base_ref, s32[256]{0:T(256)} %get-tuple-element.363.tail_ref, s32[256]{0:T(256)} %get-tuple-element.361.step_ref, s32[256,128]{1,0:T(8,128)S(1)} %copy-done.2, f32[656,128]{1,0:T(8,128)} %get-tuple-element.160.refs_0_, f32[656,128]{1,0:T(8,128)} %copy-done.57, ...), custom_call_target="tpu_custom_call" | custom-call | tf_op jit(solution)/shard_map/cond/branch_2_fun/unpack_early/pallas_call | solution.py:343
  329.2 6.1 %unpack_late.7 = f32[41,32768]{1,0:T(8,128)} custom-call(s32[1]{0:T(128)} %bitcast.2.count_ref, s32[256]{0:T(256)} %get-tuple-element.340.block_ref, s32[256]{0:T(256)} %get-tuple-element.339.base_ref, s32[256]{0:T(256)} %get-tuple-element.338.tail_ref, s32[256,128]{1,0:T(8,128)S(1)} %copy-done.2, ...), custom_call_target="tpu_custom_call", output_to_operand_aliasing={{}: (5, {})} | custom-call | tf_op jit(solution)/shard_map/cond/branch_2_fun/unpack_late/pallas_call | solution.py:423
  (146 shorter events, 74.3 us)
Async XLA Ops:
  33.6 23.9 %collective-permute-start.106 = (f32[248,128]{1,0:T(8,128)}, f32[248,128]{1,0:T(8,128)S(1)}, u32[]{:S(2)}, u32[]{:S(2)}) collective-permute-start(f32[248,128]{1,0:T(8,128)} %get-tuple-element.188), channel_id=1, source_target_pairs={{0,6},{1,7},{2,4},{3,5},{4,2},{5,3},{6,0},{7,1},{8,14},{9,15},{10,... | collective-permute-start | bytes 380936 | tf_op jit(solution)/shard_map/cond/branch_2_fun/ppermute | solution.py:497
  36.6 24.5 %collective-permute-start.107 = (f32[248,128]{1,0:T(8,128)}, f32[248,128]{1,0:T(8,128)S(1)}, u32[]{:S(2)}, u32[]{:S(2)}) collective-permute-start(f32[248,128]{1,0:T(8,128)} %get-tuple-element.189), channel_id=1, source_target_pairs={{0,7},{1,6},{2,5},{3,4},{4,3},{5,2},{6,1},{7,0},{8,15},{9,14},{10,... | collective-permute-start | bytes 380936 | tf_op jit(solution)/shard_map/cond/branch_2_fun/ppermute | solution.py:497
  37.7 33.7 %collective-permute-start.108 = (f32[248,128]{1,0:T(8,128)}, f32[248,128]{1,0:T(8,128)S(1)}, u32[]{:S(2)}, u32[]{:S(2)}) collective-permute-start(f32[248,128]{1,0:T(8,128)} %get-tuple-element.190), channel_id=1, source_target_pairs={{0,12},{1,13},{2,14},{3,15},{4,8},{5,9},{6,10},{7,11},{8,4},{9,5},... | collective-permute-start | bytes 380936 | tf_op jit(solution)/shard_map/cond/branch_2_fun/ppermute | solution.py:497
  50.3 29.3 %collective-permute-start.109 = (f32[248,128]{1,0:T(8,128)}, f32[248,128]{1,0:T(8,128)S(1)}, u32[]{:S(2)}, u32[]{:S(2)}) collective-permute-start(f32[248,128]{1,0:T(8,128)} %get-tuple-element.191), channel_id=1, source_target_pairs={{0,13},{1,12},{2,15},{3,14},{4,9},{5,8},{6,11},{7,10},{8,5},{9,4},... | collective-permute-start | bytes 380936 | tf_op jit(solution)/shard_map/cond/branch_2_fun/ppermute | solution.py:497
  53.1 27.2 %collective-permute-start.110 = (f32[248,128]{1,0:T(8,128)}, f32[248,128]{1,0:T(8,128)S(1)}, u32[]{:S(2)}, u32[]{:S(2)}) collective-permute-start(f32[248,128]{1,0:T(8,128)} %get-tuple-element.192), channel_id=1, source_target_pairs={{0,14},{1,15},{2,12},{3,13},{4,10},{5,11},{6,8},{7,9},{8,6},{9,7},... | collective-permute-start | bytes 380936 | tf_op jit(solution)/shard_map/cond/branch_2_fun/ppermute | solution.py:497
  57.5 26.4 %collective-permute-start.111 = (f32[248,128]{1,0:T(8,128)}, f32[248,128]{1,0:T(8,128)S(1)}, u32[]{:S(2)}, u32[]{:S(2)}) collective-permute-start(f32[248,128]{1,0:T(8,128)} %get-tuple-element.193), channel_id=1, source_target_pairs={{0,15},{1,14},{2,13},{3,12},{4,11},{5,10},{6,9},{7,8},{8,7},{9,6},... | collective-permute-start | bytes 380936 | tf_op jit(solution)/shard_map/cond/branch_2_fun/ppermute | solution.py:497
  61.1 25.4 %collective-permute-start.112 = (f32[248,128]{1,0:T(8,128)}, f32[248,128]{1,0:T(8,128)S(1)}, u32[]{:S(2)}, u32[]{:S(2)}) collective-permute-start(f32[248,128]{1,0:T(8,128)} %get-tuple-element.194), channel_id=1, source_target_pairs={{0,20},{1,21},{2,22},{3,23},{4,16},{5,17},{6,18},{7,19},{8,28},{9,... | collective-permute-start | bytes 380936 | tf_op jit(solution)/shard_map/cond/branch_2_fun/ppermute | solution.py:497
  72.2 106.4 %collective-permute-start.80 = (f32[656,128]{1,0:T(8,128)}, f32[656,128]{1,0:T(8,128)S(1)}, u32[]{:S(2)}, u32[]{:S(2)}) collective-permute-start(f32[656,128]{1,0:T(8,128)} %get-tuple-element.161), channel_id=1, source_target_pairs={{0,1},{1,0},{2,3},{3,2},{4,5},{5,4},{6,7},{7,6},{8,9},{9,8},{10,11... | collective-permute-start | bytes 1007624 | tf_op jit(solution)/shard_map/cond/branch_2_fun/ppermute | solution.py:497
  80.3 132.1 %collective-permute-start.95 = (f32[1888,128]{1,0:T(8,128)}, f32[1888,128]{1,0:T(8,128)S(1)}, u32[]{:S(2)}, u32[]{:S(2)}) collective-permute-start(f32[1888,128]{1,0:T(8,128)} %get-tuple-element.176), channel_id=1, source_target_pairs={{0,4},{1,5},{2,6},{3,7},{4,0},{5,1},{6,2},{7,3},{8,12},{9,13},{10,... | collective-permute-start | bytes 2899976 | tf_op jit(solution)/shard_map/cond/branch_2_fun/ppermute | solution.py:497
  80.9 132.1 %collective-permute-start.96 = (f32[1888,128]{1,0:T(8,128)}, f32[1888,128]{1,0:T(8,128)S(1)}, u32[]{:S(2)}, u32[]{:S(2)}) collective-permute-start(f32[1888,128]{1,0:T(8,128)} %get-tuple-element.177), channel_id=1, source_target_pairs={{0,6},{1,7},{2,4},{3,5},{4,2},{5,3},{6,0},{7,1},{8,14},{9,15},{10,... | collective-permute-start | bytes 2899976 | tf_op jit(solution)/shard_map/cond/branch_2_fun/ppermute | solution.py:497
  83.9 90.1 %collective-permute-start.113 = (f32[248,128]{1,0:T(8,128)S(1)}, f32[248,128]{1,0:T(8,128)S(1)}, u32[]{:S(2)}, u32[]{:S(2)}) collective-permute-start(f32[248,128]{1,0:T(8,128)S(1)} %copy-done.132), channel_id=1, source_target_pairs={{0,21},{1,20},{2,23},{3,22},{4,17},{5,16},{6,19},{7,18},{8,29},{9,... | collective-permute-start | bytes 380936 | tf_op jit(solution)/shard_map/cond/branch_2_fun/ppermute | solution.py:497
  86.5 89.3 %collective-permute-start.114 = (f32[248,128]{1,0:T(8,128)S(1)}, f32[248,128]{1,0:T(8,128)S(1)}, u32[]{:S(2)}, u32[]{:S(2)}) collective-permute-start(f32[248,128]{1,0:T(8,128)S(1)} %copy-done.131), channel_id=1, source_target_pairs={{0,22},{1,23},{2,20},{3,21},{4,18},{5,19},{6,16},{7,17},{8,30},{9,... | collective-permute-start | bytes 380936 | tf_op jit(solution)/shard_map/cond/branch_2_fun/ppermute | solution.py:497
  200.4 22.4 %collective-permute-start.87 = (f32[656,128]{1,0:T(8,128)}, f32[656,128]{1,0:T(8,128)}, u32[]{:S(2)}, u32[]{:S(2)}) collective-permute-start(f32[656,128]{1,0:T(8,128)} %get-tuple-element.168), channel_id=1, source_target_pairs={{0,16},{1,17},{2,18},{3,19},{4,20},{5,21},{6,22},{7,23},{8,24},{9,... | collective-permute-start | bytes 1007624 | tf_op jit(solution)/shard_map/cond/branch_2_fun/ppermute | solution.py:497
  212.4 23.3 %collective-permute-start.90 = (f32[656,128]{1,0:T(8,128)}, f32[656,128]{1,0:T(8,128)}, u32[]{:S(2)}, u32[]{:S(2)}) collective-permute-start(f32[656,128]{1,0:T(8,128)} %get-tuple-element.171), channel_id=1, source_target_pairs={{0,19},{1,18},{2,17},{3,16},{4,23},{5,22},{6,21},{7,20},{8,27},{9,... | collective-permute-start | bytes 1007624 | tf_op jit(solution)/shard_map/cond/branch_2_fun/ppermute | solution.py:497
  213.0 41.3 %collective-permute-start.91 = (f32[656,128]{1,0:T(8,128)}, f32[656,128]{1,0:T(8,128)}, u32[]{:S(2)}, u32[]{:S(2)}) collective-permute-start(f32[656,128]{1,0:T(8,128)} %get-tuple-element.172), channel_id=1, source_target_pairs={{0,24},{1,25},{2,26},{3,27},{4,28},{5,29},{6,30},{7,31},{8,16},{9,... | collective-permute-start | bytes 1007624 | tf_op jit(solution)/shard_map/cond/branch_2_fun/ppermute | solution.py:497
  222.9 44.4 %collective-permute-start.97 = (f32[824,128]{1,0:T(8,128)}, f32[824,128]{1,0:T(8,128)S(1)}, u32[]{:S(2)}, u32[]{:S(2)}) collective-permute-start(f32[824,128]{1,0:T(8,128)} %get-tuple-element.179), channel_id=1, source_target_pairs={{0,1},{1,0},{2,3},{3,2},{4,5},{5,4},{6,7},{7,6},{8,9},{9,8},{10,11... | collective-permute-start | bytes 1265672 | tf_op jit(solution)/shard_map/cond/branch_2_fun/ppermute | solution.py:497
  222.9 46.2 %collective-permute-start.98 = (f32[824,128]{1,0:T(8,128)}, f32[824,128]{1,0:T(8,128)S(1)}, u32[]{:S(2)}, u32[]{:S(2)}) collective-permute-start(f32[824,128]{1,0:T(8,128)} %get-tuple-element.180), channel_id=1, source_target_pairs={{0,8},{1,9},{2,10},{3,11},{4,12},{5,13},{6,14},{7,15},{8,0},{9,1},... | collective-permute-start | bytes 1265672 | tf_op jit(solution)/shard_map/cond/branch_2_fun/ppermute | solution.py:497
  224.6 32.3 %collective-permute-start.92 = (f32[656,128]{1,0:T(8,128)}, f32[656,128]{1,0:T(8,128)S(1)}, u32[]{:S(2)}, u32[]{:S(2)}) collective-permute-start(f32[656,128]{1,0:T(8,128)} %get-tuple-element.173), channel_id=1, source_target_pairs={{0,25},{1,24},{2,27},{3,26},{4,29},{5,28},{6,31},{7,30},{8,17},{9,... | collective-permute-start | bytes 1007624 | tf_op jit(solution)/shard_map/cond/branch_2_fun/ppermute | solution.py:497
  266.4 35.1 %collective-permute-start.101 = (f32[824,128]{1,0:T(8,128)}, f32[824,128]{1,0:T(8,128)S(1)}, u32[]{:S(2)}, u32[]{:S(2)}) collective-permute-start(f32[824,128]{1,0:T(8,128)} %get-tuple-element.183), channel_id=1, source_target_pairs={{0,17},{1,16},{2,19},{3,18},{4,21},{5,20},{6,23},{7,22},{8,25},{9,... | collective-permute-start | bytes 1265672 | tf_op jit(solution)/shard_map/cond/branch_2_fun/ppermute | solution.py:497
  267.3 39.4 %collective-permute-start.102 = (f32[824,128]{1,0:T(8,128)}, f32[824,128]{1,0:T(8,128)S(1)}, u32[]{:S(2)}, u32[]{:S(2)}) collective-permute-start(f32[824,128]{1,0:T(8,128)} %get-tuple-element.184), channel_id=1, source_target_pairs={{0,24},{1,25},{2,26},{3,27},{4,28},{5,29},{6,30},{7,31},{8,16},{9,... | collective-permute-start | bytes 1265672 | tf_op jit(solution)/shard_map/cond/branch_2_fun/ppermute | solution.py:497
  269.1 45.8 %collective-permute-start.103 = (f32[824,128]{1,0:T(8,128)}, f32[824,128]{1,0:T(8,128)S(1)}, u32[]{:S(2)}, u32[]{:S(2)}) collective-permute-start(f32[824,128]{1,0:T(8,128)} %get-tuple-element.185), channel_id=1, source_target_pairs={{0,25},{1,24},{2,27},{3,26},{4,29},{5,28},{6,31},{7,30},{8,17},{9,... | collective-permute-start | bytes 1265672 | tf_op jit(solution)/shard_map/cond/branch_2_fun/ppermute | solution.py:497
  275.2 53.4 %collective-permute-start.115 = (f32[248,128]{1,0:T(8,128)}, f32[248,128]{1,0:T(8,128)S(1)}, u32[]{:S(2)}, u32[]{:S(2)}) collective-permute-start(f32[248,128]{1,0:T(8,128)} %get-tuple-element.197), channel_id=1, source_target_pairs={{0,23},{1,22},{2,21},{3,20},{4,19},{5,18},{6,17},{7,16},{8,31},{9,... | collective-permute-start | bytes 380936 | tf_op jit(solution)/shard_map/cond/branch_2_fun/ppermute | solution.py:497
  280.1 48.5 %collective-permute-start.116 = (f32[248,128]{1,0:T(8,128)}, f32[248,128]{1,0:T(8,128)}, u32[]{:S(2)}, u32[]{:S(2)}) collective-permute-start(f32[248,128]{1,0:T(8,128)} %get-tuple-element.198), channel_id=1, source_target_pairs={{0,28},{1,29},{2,30},{3,31},{4,24},{5,25},{6,26},{7,27},{8,20},{9,... | collective-permute-start | bytes 380936 | tf_op jit(solution)/shard_map/cond/branch_2_fun/ppermute | solution.py:497
  301.5 27.2 %collective-permute-start.117 = (f32[248,128]{1,0:T(8,128)}, f32[248,128]{1,0:T(8,128)}, u32[]{:S(2)}, u32[]{:S(2)}) collective-permute-start(f32[248,128]{1,0:T(8,128)} %get-tuple-element.199), channel_id=1, source_target_pairs={{0,29},{1,28},{2,31},{3,30},{4,25},{5,24},{6,27},{7,26},{8,21},{9,... | collective-permute-start | bytes 380936 | tf_op jit(solution)/shard_map/cond/branch_2_fun/ppermute | solution.py:497
  (48 other events, 1569.9 us)
